TPU v7x, 32 devices: a whole 2x2x4 slice. The times are simulated.
32 devices in a mesh: gx: 4 (over y, x), gy: 2 (over core), gz: 4 (over z).
Axes of the slice: x: 2, y: 2, z: 4, core: 2. Of those that a mesh axis runs over, the one named last changes fastest.
Arguments:
- gradient: bfloat16 [32, 32, 16, 512], P(None, 'gx', 'gy', 'gz'), may hold values from -6 to 6
- noise_draw: bfloat16 [32, 32, 16, 512], P(None, 'gx', 'gy', 'gz'), may hold values from -6 to 6
- current: float32 [32, 32, 16, 512], P(None, 'gx', 'gy', 'gz'), may hold values from -6 to 6
- eigvectors: bfloat16 [32, 16, 512, 512], P('gx', 'gy', 'gz'), may hold values from -0.125 to 0.125
- eigvalues: float32 [512], replicated, may hold values from 0.05 to 50
- reaction: float32 [32, 16, 512], P('gx', 'gy', 'gz'), may hold values from 0.25 to 4
Outputs:
- proposal: float32 [32, 32, 16, 512], P(None, 'gx', 'gy', 'gz')
All inputs are finite; a program needn't handle non-finite values.
Results may differ from a plain program's by a relative error of at most 0.00031.
Values sent between devices are 32-bit elements; how exact they have to be, the bound alone decides.
A program may use at most 64 MiB of HBM per device.

v0:
```python
import jax
import jax.numpy as jnp
from jax import lax
from jax.sharding import PartitionSpec as P

SWEEPS = 4


def with_halo(block, sides, width):
    for axis, dim in sides:
        count = lax.axis_size(axis)
        forward = [(i, i + 1) for i in range(count - 1)]
        backward = [(target, source) for source, target in forward]
        low = lax.ppermute(
            lax.slice_in_dim(block, block.shape[dim] - width, None, axis=dim), axis, forward
        )
        high = lax.ppermute(lax.slice_in_dim(block, 0, width, axis=dim), axis, backward)
        block = jnp.concatenate([low, block, high], axis=dim)
    return block


def prior_root(source, reaction):
    sweeps = SWEEPS
    diagonal = reaction + 6.0
    field = source / diagonal
    for sweep_index in range(sweeps - 1):
        padded = with_halo(field, (("gx", 1), ("gy", 2), ("gz", 3)), 1)
        total = padded[:, 2:, 1:-1, 1:-1] + padded[:, :-2, 1:-1, 1:-1]
        total = total + padded[:, 1:-1, 2:, 1:-1] + padded[:, 1:-1, :-2, 1:-1]
        total = total + padded[:, 1:-1, 1:-1, 2:] + padded[:, 1:-1, 1:-1, :-2]
        field = (source + total) / diagonal
    return field


def body(gradient, noise_draw, current, eigvectors, eigvalues, reaction):
    chains = gradient.shape[0]
    rank = eigvectors.shape[3]
    cells = reaction.shape[0] * reaction.shape[1] * reaction.shape[2]
    basis = eigvectors.reshape(cells, rank)
    stacked = jnp.concatenate(
        [gradient.reshape(chains, cells), noise_draw.reshape(chains, cells)], 0
    )
    partial_sums = jnp.dot(stacked, basis, preferred_element_type=jnp.float32)
    local_part = -0.5 * gradient.astype(jnp.float32) + 1.0 * noise_draw.astype(jnp.float32)
    sums = lax.psum(partial_sums, ("gx", "gy", "gz"))
    damp = eigvalues / (eigvalues + 1.0)
    root_damp = 1.0 - 1.0 / jnp.sqrt(1.0 + eigvalues)
    coef = (0.5 * damp * sums[:chains] - 1.0 * root_damp * sums[chains:]).astype(jnp.bfloat16)
    corr = lax.dot_general(
        coef, basis, (((1,), (1,)), ((), ())), preferred_element_type=jnp.float32
    )
    field = prior_root(local_part + corr.reshape(current.shape), reaction)
    return current + field


def solution(mesh):
    return jax.shard_map(
        body,
        mesh=mesh,
        in_specs=(
            P(None, "gx", "gy", "gz"),
            P(None, "gx", "gy", "gz"),
            P(None, "gx", "gy", "gz"),
            P("gx", "gy", "gz", None),
            P(),
            P("gx", "gy", "gz"),
        ),
        out_specs=P(None, "gx", "gy", "gz"),
        check_vma=False,
    )
```

profile of v0, /device:TPU:0, one launch (start us, length us, event | category | flops | bytes accessed | tf_op | source)
XLA Modules:
  0.0 262.8 jit_solution(8625238853567087662)
XLA Ops:
  6.5 1.9 copy_bitcast_fusion
  8.4 5.7 %fusion.22 = f32[64,512]{1,0:T(8,128)} fusion(bf16[8192,512]{1,0:T(8,128)(2,1)} %bitcast.18, bf16[32,8192]{1,0:T(8,128)(2,1)S(1)} %get-tuple-element.27, bf16[32,8192]{1,0:T(8,128)(2,1)S(1)} %get-tuple-element.28), kind=kOutput, calls=%fused_computation.80 | convolution fusion | flops 538968064 | bytes 9568256 | tf_op jit(solution)/shard_map/dot_general | solution.py:43
  14.2 127.2 %all-reduce.2.cloned.1.call-done = f32[64,512]{1,0:T(8,128)} async-done(((f32[64,512]{1,0:T(8,128)}), f32[64,512]{1,0:T(8,128)}) %all-reduce.2.cloned.1.call-update) | async-done | bytes 131088 | tf_op jit(solution)/shard_map/psum | solution.py:45
  141.5 6.0 %broadcast_divide_fusion = (f32[32,8,8,128]{3,0,2,1:T(8,128)S(1)}, f32[32,8,8,128]{3,0,2,1:T(8,128)S(1)}) fusion(f32[8,8,128]{2,1,0:T(8,128)S(1)} %broadcast_add_fusion, bf16[8,8,128,512]{3,2,1,0:T(8,128)(2,1)} %param.9, f32[64,512]{1,0:T(8,128)} %all-reduce.2.cloned.1.call-done, f32[512]{0:T(512)S(1)} %get-tuple-element.24, f32[512]{0:T(512)S(1)} %get-tuple-element.23, ...), kind=kOutput, calls=%fused_computation.86 | convolution fusion | flops 270073856 | bytes 11702272 | tf_op jit(solution)/shard_map/dot_general | solution.py:49
  147.5 3.4 %collective-permute-start.1 = (f32[32,1,8,128]{3,0,2,1:T(8,128)S(1)}, f32[32,1,8,128]{3,0,2,1:T(8,128)S(1)}, u32[]{:S(2)}, u32[]{:S(2)}) collective-permute-start(f32[32,1,8,128]{3,0,2,1:T(8,128)S(1)} %get-tuple-element.21), channel_id=1, source_target_pairs={{0,8},{8,16},{16,24},{1,9},{9,17},{17,25},{2,10},{10,18},{18,26},{... | collective-permute-start | bytes 393224 | tf_op jit(solution)/shard_map/ppermute | solution.py:14
  153.4 4.7 %collective-permute-done = f32[32,1,8,128]{3,0,2,1:T(8,128)S(1)} collective-permute-done((f32[32,1,8,128]{3,0,2,1:T(8,128)S(1)}, f32[32,1,8,128]{3,0,2,1:T(8,128)S(1)}, u32[]{:S(2)}, u32[]{:S(2)}) %collective-permute-start) | collective-permute-done | bytes 131104 | tf_op jit(solution)/shard_map/ppermute | solution.py:17
  160.8 2.0 collective-permute-done.2
  163.4 2.3 fusion.37
  165.7 2.1 copy.13
  169.0 2.1 copy.15
  171.1 4.6 %collective-permute-start.5 = (f32[32,10,10,1]{0,3,2,1:T(1,128)S(1)}, f32[32,10,10,1]{0,3,2,1:T(1,128)S(1)}, u32[]{:S(2)}, u32[]{:S(2)}) collective-permute-start(f32[32,10,10,1]{0,3,2,1:T(1,128)S(1)} %copy.15), channel_id=1, source_target_pairs={{0,1},{1,2},{2,3},{4,5},{5,6},{6,7},{8,9},{9,10},{10,11},{12,13},{... | collective-permute-start | bytes 38408 | tf_op jit(solution)/shard_map/ppermute | solution.py:14
  177.5 1.9 copy.16
  179.4 2.9 %fusion.17 = f32[32,8,8,128]{3,0,2,1:T(8,128)S(1)} fusion(f32[32,8,8,128]{3,0,2,1:T(8,128)S(1)} %get-tuple-element.26, f32[32,10,10,1]{3,0,2,1:T(8,128)} %copy.16, f32[32,10,1,128]{3,0,2,1:T(8,128)} %copy-done.5, f32[32,10,1,128]{3,0,2,1:T(8,128)} %copy-done.3, f32[32,1,8,128]{3,0,2,1:T(8,128)S(1)} %collective-permute-done, ...), kind=kLoop, calls=%fused_computation.58 | loop fusion | flops 6553600 | bytes 3793920 | tf_op jit(solution)/shard_map/div | solution.py:31
  182.3 3.9 %collective-permute-start.7 = (f32[32,1,8,128]{3,0,2,1:T(8,128)S(1)}, f32[32,1,8,128]{3,0,2,1:T(8,128)S(1)}, u32[]{:S(2)}, u32[]{:S(2)}) collective-permute-start(f32[32,1,8,128]{3,0,2,1:T(8,128)S(1)} %get-tuple-element.19), channel_id=1, source_target_pairs={{0,8},{8,16},{16,24},{1,9},{9,17},{17,25},{2,10},{10,18},{18,26},{... | collective-permute-start | bytes 393224 | tf_op jit(solution)/shard_map/ppermute | solution.py:14
  188.8 4.4 %collective-permute-done.6 = f32[32,1,8,128]{3,0,2,1:T(8,128)S(1)} collective-permute-done((f32[32,1,8,128]{3,0,2,1:T(8,128)S(1)}, f32[32,1,8,128]{3,0,2,1:T(8,128)S(1)}, u32[]{:S(2)}, u32[]{:S(2)}) %collective-permute-start.6) | collective-permute-done | bytes 131104 | tf_op jit(solution)/shard_map/ppermute | solution.py:17
  195.8 2.0 collective-permute-done.8
  198.4 2.3 fusion.36
  200.7 2.1 copy.17
  204.0 2.1 copy.19
  206.1 4.8 %collective-permute-start.11 = (f32[32,10,10,1]{0,3,2,1:T(1,128)S(1)}, f32[32,10,10,1]{0,3,2,1:T(1,128)S(1)}, u32[]{:S(2)}, u32[]{:S(2)}) collective-permute-start(f32[32,10,10,1]{0,3,2,1:T(1,128)S(1)} %copy.19), channel_id=1, source_target_pairs={{0,1},{1,2},{2,3},{4,5},{5,6},{6,7},{8,9},{9,10},{10,11},{12,13},{... | collective-permute-start | bytes 38408 | tf_op jit(solution)/shard_map/ppermute | solution.py:14
  212.8 1.9 copy.20
  214.6 2.9 %fusion.10 = f32[32,8,8,128]{3,0,2,1:T(8,128)S(1)} fusion(f32[32,8,8,128]{3,0,2,1:T(8,128)S(1)} %get-tuple-element.26, f32[32,10,10,1]{3,0,2,1:T(8,128)} %copy.20, f32[32,10,1,128]{3,0,2,1:T(8,128)} %copy-done.6, f32[32,10,1,128]{3,0,2,1:T(8,128)} %copy-done.4, f32[32,1,8,128]{3,0,2,1:T(8,128)S(1)} %collective-permute-done.6, ...), kind=kLoop, calls=%fused_computation.33 | loop fusion | flops 6553600 | bytes 3793920 | tf_op jit(solution)/shard_map/div | solution.py:31
  217.5 3.4 %collective-permute-start.13 = (f32[32,1,8,128]{3,0,2,1:T(8,128)S(1)}, f32[32,1,8,128]{3,0,2,1:T(8,128)S(1)}, u32[]{:S(2)}, u32[]{:S(2)}) collective-permute-start(f32[32,1,8,128]{3,0,2,1:T(8,128)S(1)} %get-tuple-element.17), channel_id=1, source_target_pairs={{0,8},{8,16},{16,24},{1,9},{9,17},{17,25},{2,10},{10,18},{18,26},{... | collective-permute-start | bytes 393224 | tf_op jit(solution)/shard_map/ppermute | solution.py:14
  223.7 4.1 %collective-permute-done.12 = f32[32,1,8,128]{3,0,2,1:T(8,128)S(1)} collective-permute-done((f32[32,1,8,128]{3,0,2,1:T(8,128)S(1)}, f32[32,1,8,128]{3,0,2,1:T(8,128)S(1)}, u32[]{:S(2)}, u32[]{:S(2)}) %collective-permute-start.12) | collective-permute-done | bytes 131104 | tf_op jit(solution)/shard_map/ppermute | solution.py:17
  230.5 2.0 collective-permute-done.14
  233.1 2.2 fusion.35
  235.3 2.1 copy.21
  238.7 2.7 %copy.23 = f32[32,10,10,1]{0,3,2,1:T(1,128)} copy(f32[32,10,10,1]{3,0,2,1:T(8,128)} %get-tuple-element.6) | data formatting | bytes 25600 | tf_op jit(solution)/shard_map/slice | solution.py:15
  241.4 5.5 %collective-permute-start.17 = (f32[32,10,10,1]{0,3,2,1:T(1,128)}, f32[32,10,10,1]{0,3,2,1:T(1,128)}, u32[]{:S(2)}, u32[]{:S(2)}) collective-permute-start(f32[32,10,10,1]{0,3,2,1:T(1,128)} %copy.23), channel_id=1, source_target_pairs={{0,1},{1,2},{2,3},{4,5},{5,6},{6,7},{8,9},{9,10},{10,11},{12,13},{... | collective-permute-start | bytes 38408 | tf_op jit(solution)/shard_map/ppermute | solution.py:14
  246.9 1.9 copy.22
  248.8 2.6 %copy.24 = f32[32,10,10,1]{3,0,2,1:T(8,128)} copy(f32[32,10,10,1]{0,3,2,1:T(1,128)} %collective-permute-done.17) | data formatting | bytes 25600 | tf_op jit(solution)/shard_map/ppermute | solution.py:14
  251.4 3.0 %fusion.3 = f32[32,8,8,128]{3,0,2,1:T(8,128)S(1)} fusion(f32[32,8,8,128]{3,0,2,1:T(8,128)S(1)} %get-tuple-element.26, f32[32,10,10,1]{3,0,2,1:T(8,128)} %copy.24, f32[32,10,1,128]{3,0,2,1:T(8,128)} %copy-done.8, f32[32,10,1,128]{3,0,2,1:T(8,128)} %copy-done.7, f32[32,1,8,128]{3,0,2,1:T(8,128)S(1)} %collective-permute-done.12, ...), kind=kLoop, calls=%fused_computation.8 | loop fusion | flops 6815744 | bytes 4842496 | tf_op jit(solution)/shard_map/add | solution.py:53
  (62 shorter events, 26.8 us)
Async XLA Ops:
  6.5 134.9 %all-reduce.2.cloned.1.call-start = ((), (), s32[]{:S(2)}) async-start(), calls=%async_computation | async-start | bytes 262144 | tf_op jit(solution)/shard_map/psum | solution.py:45
  8.4 5.8 %copy-start.9 = (f32[8,8,128]{2,1,0:T(8,128)S(1)}, f32[8,8,128]{2,1,0:T(8,128)}, u32[]{:S(2)}) copy-start(f32[8,8,128]{2,1,0:T(8,128)} %param.11) | copy-start | bytes 98308
  8.4 5.8 %copy-start.10 = (f32[512]{0:T(512)S(1)}, f32[512]{0:T(512)}, u32[]{:S(2)}) copy-start(f32[512]{0:T(512)} %param.10) | copy-start | bytes 6148
  8.4 133.0 %copy-start = (bf16[32,8,8,128]{3,2,1,0:T(8,128)(2,1)S(1)}, bf16[32,8,8,128]{3,2,1,0:T(8,128)(2,1)}, u32[]{:S(2)}) copy-start(bf16[32,8,8,128]{3,2,1,0:T(8,128)(2,1)} %param.7) | copy-start | bytes 1572868
  8.4 133.0 %copy-start.1 = (bf16[32,8,8,128]{3,2,1,0:T(8,128)(2,1)S(1)}, bf16[32,8,8,128]{3,2,1,0:T(8,128)(2,1)}, u32[]{:S(2)}) copy-start(bf16[32,8,8,128]{3,2,1,0:T(8,128)(2,1)} %param.6) | copy-start | bytes 1572868
  147.5 5.9 %collective-permute-start.1 = (f32[32,1,8,128]{3,0,2,1:T(8,128)S(1)}, f32[32,1,8,128]{3,0,2,1:T(8,128)S(1)}, u32[]{:S(2)}, u32[]{:S(2)}) collective-permute-start(f32[32,1,8,128]{3,0,2,1:T(8,128)S(1)} %get-tuple-element.21), channel_id=1, source_target_pairs={{0,8},{8,16},{16,24},{1,9},{9,17},{17,25},{2,10},{10,18},{18,26},{... | collective-permute-start | bytes 393224 | tf_op jit(solution)/shard_map/ppermute | solution.py:14
  150.9 7.2 %collective-permute-start = (f32[32,1,8,128]{3,0,2,1:T(8,128)S(1)}, f32[32,1,8,128]{3,0,2,1:T(8,128)S(1)}, u32[]{:S(2)}, u32[]{:S(2)}) collective-permute-start(f32[32,1,8,128]{3,0,2,1:T(8,128)S(1)} %get-tuple-element.22), channel_id=1, source_target_pairs={{8,0},{16,8},{24,16},{9,1},{17,9},{25,17},{10,2},{18,10},{26,18},{... | collective-permute-start | bytes 393224 | tf_op jit(solution)/shard_map/ppermute | solution.py:17
  158.1 2.6 collective-permute-start.3
  159.5 3.3 %collective-permute-start.2 = (f32[32,10,1,128]{3,0,2,1:T(8,128)S(1)}, f32[32,10,1,128]{3,0,2,1:T(8,128)S(1)}, u32[]{:S(2)}, u32[]{:S(2)}) collective-permute-start(f32[32,10,1,128]{3,0,2,1:T(8,128)S(1)} %get-tuple-element.16), channel_id=1, source_target_pairs={{4,0},{5,1},{6,2},{7,3},{12,8},{13,9},{14,10},{15,11},{20,16},{21,... | collective-permute-start | bytes 491528 | tf_op jit(solution)/shard_map/ppermute | solution.py:17
  160.8 2.2 copy-start.3
  162.7 0.7 copy-start.5
  167.7 7.9 %collective-permute-start.4 = (f32[32,10,10,1]{0,3,2,1:T(1,128)S(1)}, f32[32,10,10,1]{0,3,2,1:T(1,128)S(1)}, u32[]{:S(2)}, u32[]{:S(2)}) collective-permute-start(f32[32,10,10,1]{0,3,2,1:T(1,128)S(1)} %copy.13), channel_id=1, source_target_pairs={{1,0},{2,1},{3,2},{5,4},{6,5},{7,6},{9,8},{10,9},{11,10},{13,12},{... | collective-permute-start | bytes 38408 | tf_op jit(solution)/shard_map/ppermute | solution.py:17
  171.1 6.4 %collective-permute-start.5 = (f32[32,10,10,1]{0,3,2,1:T(1,128)S(1)}, f32[32,10,10,1]{0,3,2,1:T(1,128)S(1)}, u32[]{:S(2)}, u32[]{:S(2)}) collective-permute-start(f32[32,10,10,1]{0,3,2,1:T(1,128)S(1)} %copy.15), channel_id=1, source_target_pairs={{0,1},{1,2},{2,3},{4,5},{5,6},{6,7},{8,9},{9,10},{10,11},{12,13},{... | collective-permute-start | bytes 38408 | tf_op jit(solution)/shard_map/ppermute | solution.py:14
  182.3 6.4 %collective-permute-start.7 = (f32[32,1,8,128]{3,0,2,1:T(8,128)S(1)}, f32[32,1,8,128]{3,0,2,1:T(8,128)S(1)}, u32[]{:S(2)}, u32[]{:S(2)}) collective-permute-start(f32[32,1,8,128]{3,0,2,1:T(8,128)S(1)} %get-tuple-element.19), channel_id=1, source_target_pairs={{0,8},{8,16},{16,24},{1,9},{9,17},{17,25},{2,10},{10,18},{18,26},{... | collective-permute-start | bytes 393224 | tf_op jit(solution)/shard_map/ppermute | solution.py:14
  186.3 6.9 %collective-permute-start.6 = (f32[32,1,8,128]{3,0,2,1:T(8,128)S(1)}, f32[32,1,8,128]{3,0,2,1:T(8,128)S(1)}, u32[]{:S(2)}, u32[]{:S(2)}) collective-permute-start(f32[32,1,8,128]{3,0,2,1:T(8,128)S(1)} %get-tuple-element.20), channel_id=1, source_target_pairs={{8,0},{16,8},{24,16},{9,1},{17,9},{25,17},{10,2},{18,10},{26,18},{... | collective-permute-start | bytes 393224 | tf_op jit(solution)/shard_map/ppermute | solution.py:17
  193.2 2.6 collective-permute-start.9
  194.5 3.3 %collective-permute-start.8 = (f32[32,10,1,128]{3,0,2,1:T(8,128)S(1)}, f32[32,10,1,128]{3,0,2,1:T(8,128)S(1)}, u32[]{:S(2)}, u32[]{:S(2)}) collective-permute-start(f32[32,10,1,128]{3,0,2,1:T(8,128)S(1)} %get-tuple-element.14), channel_id=1, source_target_pairs={{4,0},{5,1},{6,2},{7,3},{12,8},{13,9},{14,10},{15,11},{20,16},{21,... | collective-permute-start | bytes 491528 | tf_op jit(solution)/shard_map/ppermute | solution.py:17
  195.8 2.2 copy-start.4
  197.8 0.7 copy-start.6
  202.7 8.2 %collective-permute-start.10 = (f32[32,10,10,1]{0,3,2,1:T(1,128)S(1)}, f32[32,10,10,1]{0,3,2,1:T(1,128)S(1)}, u32[]{:S(2)}, u32[]{:S(2)}) collective-permute-start(f32[32,10,10,1]{0,3,2,1:T(1,128)S(1)} %copy.17), channel_id=1, source_target_pairs={{1,0},{2,1},{3,2},{5,4},{6,5},{7,6},{9,8},{10,9},{11,10},{13,12},{... | collective-permute-start | bytes 38408 | tf_op jit(solution)/shard_map/ppermute | solution.py:17
  206.1 6.6 %collective-permute-start.11 = (f32[32,10,10,1]{0,3,2,1:T(1,128)S(1)}, f32[32,10,10,1]{0,3,2,1:T(1,128)S(1)}, u32[]{:S(2)}, u32[]{:S(2)}) collective-permute-start(f32[32,10,10,1]{0,3,2,1:T(1,128)S(1)} %copy.19), channel_id=1, source_target_pairs={{0,1},{1,2},{2,3},{4,5},{5,6},{6,7},{8,9},{9,10},{10,11},{12,13},{... | collective-permute-start | bytes 38408 | tf_op jit(solution)/shard_map/ppermute | solution.py:14
  217.5 6.1 %collective-permute-start.13 = (f32[32,1,8,128]{3,0,2,1:T(8,128)S(1)}, f32[32,1,8,128]{3,0,2,1:T(8,128)S(1)}, u32[]{:S(2)}, u32[]{:S(2)}) collective-permute-start(f32[32,1,8,128]{3,0,2,1:T(8,128)S(1)} %get-tuple-element.17), channel_id=1, source_target_pairs={{0,8},{8,16},{16,24},{1,9},{9,17},{17,25},{2,10},{10,18},{18,26},{... | collective-permute-start | bytes 393224 | tf_op jit(solution)/shard_map/ppermute | solution.py:14
  220.9 6.9 %collective-permute-start.12 = (f32[32,1,8,128]{3,0,2,1:T(8,128)S(1)}, f32[32,1,8,128]{3,0,2,1:T(8,128)S(1)}, u32[]{:S(2)}, u32[]{:S(2)}) collective-permute-start(f32[32,1,8,128]{3,0,2,1:T(8,128)S(1)} %get-tuple-element.18), channel_id=1, source_target_pairs={{8,0},{16,8},{24,16},{9,1},{17,9},{25,17},{10,2},{18,10},{26,18},{... | collective-permute-start | bytes 393224 | tf_op jit(solution)/shard_map/ppermute | solution.py:17
  227.8 2.6 collective-permute-start.15
  229.1 3.3 %collective-permute-start.14 = (f32[32,10,1,128]{3,0,2,1:T(8,128)S(1)}, f32[32,10,1,128]{3,0,2,1:T(8,128)S(1)}, u32[]{:S(2)}, u32[]{:S(2)}) collective-permute-start(f32[32,10,1,128]{3,0,2,1:T(8,128)S(1)} %get-tuple-element.12), channel_id=1, source_target_pairs={{4,0},{5,1},{6,2},{7,3},{12,8},{13,9},{14,10},{15,11},{20,16},{21,... | collective-permute-start | bytes 491528 | tf_op jit(solution)/shard_map/ppermute | solution.py:17
  230.4 2.2 copy-start.7
  232.4 0.7 copy-start.8
  237.4 9.5 %collective-permute-start.16 = (f32[32,10,10,1]{0,3,2,1:T(1,128)S(1)}, f32[32,10,10,1]{0,3,2,1:T(1,128)S(1)}, u32[]{:S(2)}, u32[]{:S(2)}) collective-permute-start(f32[32,10,10,1]{0,3,2,1:T(1,128)S(1)} %copy.21), channel_id=1, source_target_pairs={{1,0},{2,1},{3,2},{5,4},{6,5},{7,6},{9,8},{10,9},{11,10},{13,12},{... | collective-permute-start | bytes 38408 | tf_op jit(solution)/shard_map/ppermute | solution.py:17
  241.4 10.0 %copy-start.2 = (f32[32,8,8,128]{3,2,1,0:T(8,128)S(1)}, f32[32,8,8,128]{3,2,1,0:T(8,128)}, u32[]{:S(2)}) copy-start(f32[32,8,8,128]{3,2,1,0:T(8,128)} %param.8) | copy-start | bytes 3145732
  241.4 7.4 %collective-permute-start.17 = (f32[32,10,10,1]{0,3,2,1:T(1,128)}, f32[32,10,10,1]{0,3,2,1:T(1,128)}, u32[]{:S(2)}, u32[]{:S(2)}) collective-permute-start(f32[32,10,10,1]{0,3,2,1:T(1,128)} %copy.23), channel_id=1, source_target_pairs={{0,1},{1,2},{2,3},{4,5},{5,6},{6,7},{8,9},{9,10},{10,11},{12,13},{... | collective-permute-start | bytes 38408 | tf_op jit(solution)/shard_map/ppermute | solution.py:14
Sparse Core Ops, SparseCore 0:
  14.3 127.1 all-reduce.1
where the time goes:
time: 264 us; the launch traced here: 263 us
  waiting for transfers between devices  150 us (57%)
  starting transfers between devices  41.1 us (16%)
  local copies, waits for them, and re-layouts  36.7 us (14%)
  between operations  13.8 us (5%)
  matrix products  11.7 us (4%)
  other arithmetic  9.37 us (4%)
    psum x1, waiting for transfers between devices, body(): sums = lax.psum(partial_sums, ('gx', 'gy', 'gz'))  127 us
    ppermute x9, starting transfers between devices, with_halo(): lax.ppermute(lax.slice_in_dim(block, block.shape[dim] - width, None, axis...  29.4 us
    ppermute x9, waiting for transfers between devices, with_halo(): lax.ppermute(lax.slice_in_dim(block, 0, width, axis=dim), axis, backward)  19.1 us
    slice x6, local copies, waits for them, and re-layouts, with_halo(): lax.slice_in_dim(block, 0, width, axis=dim)  13 us
    ppermute x9, starting transfers between devices, with_halo(): lax.ppermute(lax.slice_in_dim(block, 0, width, axis=dim), axis, backward)  11.6 us
    slice x6, local copies, waits for them, and re-layouts, with_halo(): lax.slice_in_dim(block, block.shape[dim] - width, None, axis=dim)  6.9 us
    ppermute x3, local copies, waits for them, and re-layouts, with_halo(): lax.ppermute(lax.slice_in_dim(block, block.shape[dim] - width, None, axis...  6.34 us
    dot_general x1, matrix products, body(): lax.dot_general(coef, basis, (((1,), (1,)), ((), ())), preferred_element_...  6.04 us
  transfers between devices with their start and end apart: 19, of which 10 were waited for; matrix products, arithmetic and copies ran while one was open for 5% of the time, Pallas kernels for 0%

commit v1 on v0

--- a/solution.py
+++ b/solution.py
@@ -42,7 +42,9 @@
     )
     partial_sums = jnp.dot(stacked, basis, preferred_element_type=jnp.float32)
     local_part = -0.5 * gradient.astype(jnp.float32) + 1.0 * noise_draw.astype(jnp.float32)
-    sums = lax.psum(partial_sums, ("gx", "gy", "gz"))
+    sums = partial_sums
+    for u in (("gy", "gz"), "gx"):
+        sums = lax.psum(sums, u)
     damp = eigvalues / (eigvalues + 1.0)
     root_damp = 1.0 - 1.0 / jnp.sqrt(1.0 + eigvalues)
     coef = (0.5 * damp * sums[:chains] - 1.0 * root_damp * sums[chains:]).astype(jnp.bfloat16)

time: 264 us -> 238 us (0.902)
  waiting for transfers between devices: 150 us -> 125 us
    psum x1 -> x2, waiting for transfers between devices: 127 us -> 102 us  [body(): sums = lax.psum(sums, u)]
  transfers between devices with their start and end apart: 19 -> 20, of which waited for: 10 -> 11; matrix products, arithmetic and copies ran while one was open for 5% -> 5% of each run, Pallas kernels for 0% -> 0%
where the time goes in v1:
time: 238 us; the launch traced here: 237 us
  waiting for transfers between devices  125 us (53%)
  starting transfers between devices  40.5 us (17%)
  local copies, waits for them, and re-layouts  36.8 us (15%)
  between operations  13.8 us (6%)
  matrix products  11.7 us (5%)
  other arithmetic  9.38 us (4%)
    psum x2, waiting for transfers between devices, body(): sums = lax.psum(sums, u)  102 us
    ppermute x9, starting transfers between devices, with_halo(): lax.ppermute(lax.slice_in_dim(block, block.shape[dim] - width, None, axis...  28.9 us
    ppermute x9, waiting for transfers between devices, with_halo(): lax.ppermute(lax.slice_in_dim(block, 0, width, axis=dim), axis, backward)  19 us
    slice x6, local copies, waits for them, and re-layouts, with_halo(): lax.slice_in_dim(block, 0, width, axis=dim)  13 us
    ppermute x9, starting transfers between devices, with_halo(): lax.ppermute(lax.slice_in_dim(block, 0, width, axis=dim), axis, backward)  11.6 us
    slice x6, local copies, waits for them, and re-layouts, with_halo(): lax.slice_in_dim(block, block.shape[dim] - width, None, axis=dim)  6.9 us
    ppermute x3, local copies, waits for them, and re-layouts, with_halo(): lax.ppermute(lax.slice_in_dim(block, block.shape[dim] - width, None, axis...  6.34 us
    dot_general x1, matrix products, body(): lax.dot_general(coef, basis, (((1,), (1,)), ((), ())), preferred_element_...  6.05 us
  transfers between devices with their start and end apart: 20, of which 11 were waited for; matrix products, arithmetic and copies ran while one was open for 5% of the time, Pallas kernels for 0%

profile of v1, /device:TPU:0, one launch (start us, length us, event | category | flops | bytes accessed | tf_op | source)
XLA Modules:
  0.0 237.1 jit_solution(12538210373431239612)
XLA Ops:
  6.5 1.9 copy_bitcast_fusion
  8.4 5.7 %fusion.22 = f32[64,512]{1,0:T(8,128)} fusion(bf16[8192,512]{1,0:T(8,128)(2,1)} %bitcast.18, bf16[32,8192]{1,0:T(8,128)(2,1)S(1)} %get-tuple-element.27, bf16[32,8192]{1,0:T(8,128)(2,1)S(1)} %get-tuple-element.28), kind=kOutput, calls=%fused_computation.80 | convolution fusion | flops 538968064 | bytes 9568256 | tf_op jit(solution)/shard_map/dot_general | solution.py:43
  14.2 57.8 %all-reduce.3.cloned.1.call-done = f32[64,512]{1,0:T(8,128)} async-done(((f32[64,512]{1,0:T(8,128)}), f32[64,512]{1,0:T(8,128)}) %all-reduce.3.cloned.1.call-update) | async-done | bytes 131088 | tf_op jit(solution)/shard_map/psum | solution.py:47
  72.1 44.1 %all-reduce.5.cloned.1.call-done = f32[64,512]{1,0:T(8,128)} async-done(((f32[64,512]{1,0:T(8,128)}), f32[64,512]{1,0:T(8,128)}) %all-reduce.5.cloned.1.call-update) | async-done | bytes 131088 | tf_op jit(solution)/shard_map/psum | solution.py:47
  116.2 6.0 %broadcast_divide_fusion = (f32[32,8,8,128]{3,0,2,1:T(8,128)S(1)}, f32[32,8,8,128]{3,0,2,1:T(8,128)S(1)}) fusion(f32[8,8,128]{2,1,0:T(8,128)S(1)} %broadcast_add_fusion, bf16[8,8,128,512]{3,2,1,0:T(8,128)(2,1)} %param.9, f32[64,512]{1,0:T(8,128)} %all-reduce.5.cloned.1.call-done, f32[512]{0:T(512)S(1)} %get-tuple-element.24, f32[512]{0:T(512)S(1)} %get-tuple-element.23, ...), kind=kOutput, calls=%fused_computation.86 | convolution fusion | flops 270073856 | bytes 11702272 | tf_op jit(solution)/shard_map/dot_general | solution.py:51
  122.3 3.4 %collective-permute-start.1 = (f32[32,1,8,128]{3,0,2,1:T(8,128)S(1)}, f32[32,1,8,128]{3,0,2,1:T(8,128)S(1)}, u32[]{:S(2)}, u32[]{:S(2)}) collective-permute-start(f32[32,1,8,128]{3,0,2,1:T(8,128)S(1)} %get-tuple-element.21), channel_id=1, source_target_pairs={{0,8},{8,16},{16,24},{1,9},{9,17},{17,25},{2,10},{10,18},{18,26},{... | collective-permute-start | bytes 393224 | tf_op jit(solution)/shard_map/ppermute | solution.py:14
  128.2 4.6 %collective-permute-done = f32[32,1,8,128]{3,0,2,1:T(8,128)S(1)} collective-permute-done((f32[32,1,8,128]{3,0,2,1:T(8,128)S(1)}, f32[32,1,8,128]{3,0,2,1:T(8,128)S(1)}, u32[]{:S(2)}, u32[]{:S(2)}) %collective-permute-start) | collective-permute-done | bytes 131104 | tf_op jit(solution)/shard_map/ppermute | solution.py:17
  135.5 2.0 collective-permute-done.2
  138.1 2.3 fusion.37
  140.3 2.1 copy.13
  143.7 2.1 copy.15
  145.8 4.6 %collective-permute-start.5 = (f32[32,10,10,1]{0,3,2,1:T(1,128)S(1)}, f32[32,10,10,1]{0,3,2,1:T(1,128)S(1)}, u32[]{:S(2)}, u32[]{:S(2)}) collective-permute-start(f32[32,10,10,1]{0,3,2,1:T(1,128)S(1)} %copy.15), channel_id=1, source_target_pairs={{0,1},{1,2},{2,3},{4,5},{5,6},{6,7},{8,9},{9,10},{10,11},{12,13},{... | collective-permute-start | bytes 38408 | tf_op jit(solution)/shard_map/ppermute | solution.py:14
  152.2 1.9 copy.16
  154.1 2.9 %fusion.17 = f32[32,8,8,128]{3,0,2,1:T(8,128)S(1)} fusion(f32[32,8,8,128]{3,0,2,1:T(8,128)S(1)} %get-tuple-element.26, f32[32,10,10,1]{3,0,2,1:T(8,128)} %copy.16, f32[32,10,1,128]{3,0,2,1:T(8,128)} %copy-done.5, f32[32,10,1,128]{3,0,2,1:T(8,128)} %copy-done.3, f32[32,1,8,128]{3,0,2,1:T(8,128)S(1)} %collective-permute-done, ...), kind=kLoop, calls=%fused_computation.58 | loop fusion | flops 6553600 | bytes 3793920 | tf_op jit(solution)/shard_map/div | solution.py:31
  157.0 3.9 %collective-permute-start.7 = (f32[32,1,8,128]{3,0,2,1:T(8,128)S(1)}, f32[32,1,8,128]{3,0,2,1:T(8,128)S(1)}, u32[]{:S(2)}, u32[]{:S(2)}) collective-permute-start(f32[32,1,8,128]{3,0,2,1:T(8,128)S(1)} %get-tuple-element.19), channel_id=1, source_target_pairs={{0,8},{8,16},{16,24},{1,9},{9,17},{17,25},{2,10},{10,18},{18,26},{... | collective-permute-start | bytes 393224 | tf_op jit(solution)/shard_map/ppermute | solution.py:14
  163.4 4.4 %collective-permute-done.6 = f32[32,1,8,128]{3,0,2,1:T(8,128)S(1)} collective-permute-done((f32[32,1,8,128]{3,0,2,1:T(8,128)S(1)}, f32[32,1,8,128]{3,0,2,1:T(8,128)S(1)}, u32[]{:S(2)}, u32[]{:S(2)}) %collective-permute-start.6) | collective-permute-done | bytes 131104 | tf_op jit(solution)/shard_map/ppermute | solution.py:17
  170.5 2.0 collective-permute-done.8
  173.3 2.3 fusion.36
  175.5 2.1 copy.17
  178.9 2.1 copy.19
  181.0 4.8 %collective-permute-start.11 = (f32[32,10,10,1]{0,3,2,1:T(1,128)S(1)}, f32[32,10,10,1]{0,3,2,1:T(1,128)S(1)}, u32[]{:S(2)}, u32[]{:S(2)}) collective-permute-start(f32[32,10,10,1]{0,3,2,1:T(1,128)S(1)} %copy.19), channel_id=1, source_target_pairs={{0,1},{1,2},{2,3},{4,5},{5,6},{6,7},{8,9},{9,10},{10,11},{12,13},{... | collective-permute-start | bytes 38408 | tf_op jit(solution)/shard_map/ppermute | solution.py:14
  187.6 1.9 copy.20
  189.5 2.9 %fusion.10 = f32[32,8,8,128]{3,0,2,1:T(8,128)S(1)} fusion(f32[32,8,8,128]{3,0,2,1:T(8,128)S(1)} %get-tuple-element.26, f32[32,10,10,1]{3,0,2,1:T(8,128)} %copy.20, f32[32,10,1,128]{3,0,2,1:T(8,128)} %copy-done.6, f32[32,10,1,128]{3,0,2,1:T(8,128)} %copy-done.4, f32[32,1,8,128]{3,0,2,1:T(8,128)S(1)} %collective-permute-done.6, ...), kind=kLoop, calls=%fused_computation.33 | loop fusion | flops 6553600 | bytes 3793920 | tf_op jit(solution)/shard_map/div | solution.py:31
  192.4 2.8 %collective-permute-start.13 = (f32[32,1,8,128]{3,0,2,1:T(8,128)S(1)}, f32[32,1,8,128]{3,0,2,1:T(8,128)S(1)}, u32[]{:S(2)}, u32[]{:S(2)}) collective-permute-start(f32[32,1,8,128]{3,0,2,1:T(8,128)S(1)} %get-tuple-element.17), channel_id=1, source_target_pairs={{0,8},{8,16},{16,24},{1,9},{9,17},{17,25},{2,10},{10,18},{18,26},{... | collective-permute-start | bytes 393224 | tf_op jit(solution)/shard_map/ppermute | solution.py:14
  198.0 4.1 %collective-permute-done.12 = f32[32,1,8,128]{3,0,2,1:T(8,128)S(1)} collective-permute-done((f32[32,1,8,128]{3,0,2,1:T(8,128)S(1)}, f32[32,1,8,128]{3,0,2,1:T(8,128)S(1)}, u32[]{:S(2)}, u32[]{:S(2)}) %collective-permute-start.12) | collective-permute-done | bytes 131104 | tf_op jit(solution)/shard_map/ppermute | solution.py:17
  204.8 2.0 collective-permute-done.14
  207.4 2.2 fusion.35
  209.7 2.1 copy.21
  213.0 2.7 %copy.23 = f32[32,10,10,1]{0,3,2,1:T(1,128)} copy(f32[32,10,10,1]{3,0,2,1:T(8,128)} %get-tuple-element.6) | data formatting | bytes 25600 | tf_op jit(solution)/shard_map/slice | solution.py:15
  215.7 5.5 %collective-permute-start.17 = (f32[32,10,10,1]{0,3,2,1:T(1,128)}, f32[32,10,10,1]{0,3,2,1:T(1,128)}, u32[]{:S(2)}, u32[]{:S(2)}) collective-permute-start(f32[32,10,10,1]{0,3,2,1:T(1,128)} %copy.23), channel_id=1, source_target_pairs={{0,1},{1,2},{2,3},{4,5},{5,6},{6,7},{8,9},{9,10},{10,11},{12,13},{... | collective-permute-start | bytes 38408 | tf_op jit(solution)/shard_map/ppermute | solution.py:14
  223.1 2.6 %copy.24 = f32[32,10,10,1]{3,0,2,1:T(8,128)} copy(f32[32,10,10,1]{0,3,2,1:T(1,128)} %collective-permute-done.17) | data formatting | bytes 25600 | tf_op jit(solution)/shard_map/ppermute | solution.py:14
  225.7 3.0 %fusion.3 = f32[32,8,8,128]{3,0,2,1:T(8,128)S(1)} fusion(f32[32,8,8,128]{3,0,2,1:T(8,128)S(1)} %get-tuple-element.26, f32[32,10,10,1]{3,0,2,1:T(8,128)} %copy.24, f32[32,10,1,128]{3,0,2,1:T(8,128)} %copy-done.8, f32[32,10,1,128]{3,0,2,1:T(8,128)} %copy-done.7, f32[32,1,8,128]{3,0,2,1:T(8,128)S(1)} %collective-permute-done.12, ...), kind=kLoop, calls=%fused_computation.8 | loop fusion | flops 6815744 | bytes 4842496 | tf_op jit(solution)/shard_map/add | solution.py:55
  (65 shorter events, 28.9 us)
Async XLA Ops:
  6.5 65.5 %all-reduce.3.cloned.1.call-start = ((), (), s32[]{:S(2)}) async-start(), calls=%async_computation | async-start | bytes 262144 | tf_op jit(solution)/shard_map/psum | solution.py:47
  8.4 5.8 %copy-start.9 = (f32[8,8,128]{2,1,0:T(8,128)S(1)}, f32[8,8,128]{2,1,0:T(8,128)}, u32[]{:S(2)}) copy-start(f32[8,8,128]{2,1,0:T(8,128)} %param.11) | copy-start | bytes 98308
  8.4 63.6 %copy-start.10 = (f32[512]{0:T(512)S(1)}, f32[512]{0:T(512)}, u32[]{:S(2)}) copy-start(f32[512]{0:T(512)} %param.10) | copy-start | bytes 6148
  8.4 107.8 %copy-start = (bf16[32,8,8,128]{3,2,1,0:T(8,128)(2,1)S(1)}, bf16[32,8,8,128]{3,2,1,0:T(8,128)(2,1)}, u32[]{:S(2)}) copy-start(bf16[32,8,8,128]{3,2,1,0:T(8,128)(2,1)} %param.7) | copy-start | bytes 1572868
  8.4 107.8 %copy-start.1 = (bf16[32,8,8,128]{3,2,1,0:T(8,128)(2,1)S(1)}, bf16[32,8,8,128]{3,2,1,0:T(8,128)(2,1)}, u32[]{:S(2)}) copy-start(bf16[32,8,8,128]{3,2,1,0:T(8,128)(2,1)} %param.6) | copy-start | bytes 1572868
  14.2 102.0 %all-reduce.5.cloned.1.call-start = ((), (), s32[]{:S(2)}) async-start(), calls=%async_computation.1 | async-start | bytes 262144 | tf_op jit(solution)/shard_map/psum | solution.py:47
  122.3 5.9 %collective-permute-start.1 = (f32[32,1,8,128]{3,0,2,1:T(8,128)S(1)}, f32[32,1,8,128]{3,0,2,1:T(8,128)S(1)}, u32[]{:S(2)}, u32[]{:S(2)}) collective-permute-start(f32[32,1,8,128]{3,0,2,1:T(8,128)S(1)} %get-tuple-element.21), channel_id=1, source_target_pairs={{0,8},{8,16},{16,24},{1,9},{9,17},{17,25},{2,10},{10,18},{18,26},{... | collective-permute-start | bytes 393224 | tf_op jit(solution)/shard_map/ppermute | solution.py:14
  125.7 7.1 %collective-permute-start = (f32[32,1,8,128]{3,0,2,1:T(8,128)S(1)}, f32[32,1,8,128]{3,0,2,1:T(8,128)S(1)}, u32[]{:S(2)}, u32[]{:S(2)}) collective-permute-start(f32[32,1,8,128]{3,0,2,1:T(8,128)S(1)} %get-tuple-element.22), channel_id=1, source_target_pairs={{8,0},{16,8},{24,16},{9,1},{17,9},{25,17},{10,2},{18,10},{26,18},{... | collective-permute-start | bytes 393224 | tf_op jit(solution)/shard_map/ppermute | solution.py:17
  132.8 2.6 %collective-permute-start.3 = (f32[32,10,1,128]{3,0,2,1:T(8,128)S(1)}, f32[32,10,1,128]{3,0,2,1:T(8,128)S(1)}, u32[]{:S(2)}, u32[]{:S(2)}) collective-permute-start(f32[32,10,1,128]{3,0,2,1:T(8,128)S(1)} %get-tuple-element.15), channel_id=1, source_target_pairs={{0,4},{1,5},{2,6},{3,7},{8,12},{9,13},{10,14},{11,15},{16,20},{17,... | collective-permute-start | bytes 491528 | tf_op jit(solution)/shard_map/ppermute | solution.py:14
  134.1 3.3 %collective-permute-start.2 = (f32[32,10,1,128]{3,0,2,1:T(8,128)S(1)}, f32[32,10,1,128]{3,0,2,1:T(8,128)S(1)}, u32[]{:S(2)}, u32[]{:S(2)}) collective-permute-start(f32[32,10,1,128]{3,0,2,1:T(8,128)S(1)} %get-tuple-element.16), channel_id=1, source_target_pairs={{4,0},{5,1},{6,2},{7,3},{12,8},{13,9},{14,10},{15,11},{20,16},{21,... | collective-permute-start | bytes 491528 | tf_op jit(solution)/shard_map/ppermute | solution.py:17
  135.4 2.2 copy-start.3
  137.4 0.7 copy-start.5
  142.4 7.9 %collective-permute-start.4 = (f32[32,10,10,1]{0,3,2,1:T(1,128)S(1)}, f32[32,10,10,1]{0,3,2,1:T(1,128)S(1)}, u32[]{:S(2)}, u32[]{:S(2)}) collective-permute-start(f32[32,10,10,1]{0,3,2,1:T(1,128)S(1)} %copy.13), channel_id=1, source_target_pairs={{1,0},{2,1},{3,2},{5,4},{6,5},{7,6},{9,8},{10,9},{11,10},{13,12},{... | collective-permute-start | bytes 38408 | tf_op jit(solution)/shard_map/ppermute | solution.py:17
  145.8 6.4 %collective-permute-start.5 = (f32[32,10,10,1]{0,3,2,1:T(1,128)S(1)}, f32[32,10,10,1]{0,3,2,1:T(1,128)S(1)}, u32[]{:S(2)}, u32[]{:S(2)}) collective-permute-start(f32[32,10,10,1]{0,3,2,1:T(1,128)S(1)} %copy.15), channel_id=1, source_target_pairs={{0,1},{1,2},{2,3},{4,5},{5,6},{6,7},{8,9},{9,10},{10,11},{12,13},{... | collective-permute-start | bytes 38408 | tf_op jit(solution)/shard_map/ppermute | solution.py:14
  157.0 6.4 %collective-permute-start.7 = (f32[32,1,8,128]{3,0,2,1:T(8,128)S(1)}, f32[32,1,8,128]{3,0,2,1:T(8,128)S(1)}, u32[]{:S(2)}, u32[]{:S(2)}) collective-permute-start(f32[32,1,8,128]{3,0,2,1:T(8,128)S(1)} %get-tuple-element.19), channel_id=1, source_target_pairs={{0,8},{8,16},{16,24},{1,9},{9,17},{17,25},{2,10},{10,18},{18,26},{... | collective-permute-start | bytes 393224 | tf_op jit(solution)/shard_map/ppermute | solution.py:14
  160.9 6.9 %collective-permute-start.6 = (f32[32,1,8,128]{3,0,2,1:T(8,128)S(1)}, f32[32,1,8,128]{3,0,2,1:T(8,128)S(1)}, u32[]{:S(2)}, u32[]{:S(2)}) collective-permute-start(f32[32,1,8,128]{3,0,2,1:T(8,128)S(1)} %get-tuple-element.20), channel_id=1, source_target_pairs={{8,0},{16,8},{24,16},{9,1},{17,9},{25,17},{10,2},{18,10},{26,18},{... | collective-permute-start | bytes 393224 | tf_op jit(solution)/shard_map/ppermute | solution.py:17
  167.8 2.6 %collective-permute-start.9 = (f32[32,10,1,128]{3,0,2,1:T(8,128)S(1)}, f32[32,10,1,128]{3,0,2,1:T(8,128)S(1)}, u32[]{:S(2)}, u32[]{:S(2)}) collective-permute-start(f32[32,10,1,128]{3,0,2,1:T(8,128)S(1)} %get-tuple-element.13), channel_id=1, source_target_pairs={{0,4},{1,5},{2,6},{3,7},{8,12},{9,13},{10,14},{11,15},{16,20},{17,... | collective-permute-start | bytes 491528 | tf_op jit(solution)/shard_map/ppermute | solution.py:14
  169.1 3.3 %collective-permute-start.8 = (f32[32,10,1,128]{3,0,2,1:T(8,128)S(1)}, f32[32,10,1,128]{3,0,2,1:T(8,128)S(1)}, u32[]{:S(2)}, u32[]{:S(2)}) collective-permute-start(f32[32,10,1,128]{3,0,2,1:T(8,128)S(1)} %get-tuple-element.14), channel_id=1, source_target_pairs={{4,0},{5,1},{6,2},{7,3},{12,8},{13,9},{14,10},{15,11},{20,16},{21,... | collective-permute-start | bytes 491528 | tf_op jit(solution)/shard_map/ppermute | solution.py:17
  170.5 2.0 copy-start.4
  172.4 0.7 copy-start.6
  177.6 8.2 %collective-permute-start.10 = (f32[32,10,10,1]{0,3,2,1:T(1,128)S(1)}, f32[32,10,10,1]{0,3,2,1:T(1,128)S(1)}, u32[]{:S(2)}, u32[]{:S(2)}) collective-permute-start(f32[32,10,10,1]{0,3,2,1:T(1,128)S(1)} %copy.17), channel_id=1, source_target_pairs={{1,0},{2,1},{3,2},{5,4},{6,5},{7,6},{9,8},{10,9},{11,10},{13,12},{... | collective-permute-start | bytes 38408 | tf_op jit(solution)/shard_map/ppermute | solution.py:17
  181.0 6.6 %collective-permute-start.11 = (f32[32,10,10,1]{0,3,2,1:T(1,128)S(1)}, f32[32,10,10,1]{0,3,2,1:T(1,128)S(1)}, u32[]{:S(2)}, u32[]{:S(2)}) collective-permute-start(f32[32,10,10,1]{0,3,2,1:T(1,128)S(1)} %copy.19), channel_id=1, source_target_pairs={{0,1},{1,2},{2,3},{4,5},{5,6},{6,7},{8,9},{9,10},{10,11},{12,13},{... | collective-permute-start | bytes 38408 | tf_op jit(solution)/shard_map/ppermute | solution.py:14
  192.4 5.6 %collective-permute-start.13 = (f32[32,1,8,128]{3,0,2,1:T(8,128)S(1)}, f32[32,1,8,128]{3,0,2,1:T(8,128)S(1)}, u32[]{:S(2)}, u32[]{:S(2)}) collective-permute-start(f32[32,1,8,128]{3,0,2,1:T(8,128)S(1)} %get-tuple-element.17), channel_id=1, source_target_pairs={{0,8},{8,16},{16,24},{1,9},{9,17},{17,25},{2,10},{10,18},{18,26},{... | collective-permute-start | bytes 393224 | tf_op jit(solution)/shard_map/ppermute | solution.py:14
  195.2 6.9 %collective-permute-start.12 = (f32[32,1,8,128]{3,0,2,1:T(8,128)S(1)}, f32[32,1,8,128]{3,0,2,1:T(8,128)S(1)}, u32[]{:S(2)}, u32[]{:S(2)}) collective-permute-start(f32[32,1,8,128]{3,0,2,1:T(8,128)S(1)} %get-tuple-element.18), channel_id=1, source_target_pairs={{8,0},{16,8},{24,16},{9,1},{17,9},{25,17},{10,2},{18,10},{26,18},{... | collective-permute-start | bytes 393224 | tf_op jit(solution)/shard_map/ppermute | solution.py:17
  202.2 2.6 %collective-permute-start.15 = (f32[32,10,1,128]{3,0,2,1:T(8,128)S(1)}, f32[32,10,1,128]{3,0,2,1:T(8,128)S(1)}, u32[]{:S(2)}, u32[]{:S(2)}) collective-permute-start(f32[32,10,1,128]{3,0,2,1:T(8,128)S(1)} %get-tuple-element.11), channel_id=1, source_target_pairs={{0,4},{1,5},{2,6},{3,7},{8,12},{9,13},{10,14},{11,15},{16,20},{17,... | collective-permute-start | bytes 491528 | tf_op jit(solution)/shard_map/ppermute | solution.py:14
  203.5 3.3 %collective-permute-start.14 = (f32[32,10,1,128]{3,0,2,1:T(8,128)S(1)}, f32[32,10,1,128]{3,0,2,1:T(8,128)S(1)}, u32[]{:S(2)}, u32[]{:S(2)}) collective-permute-start(f32[32,10,1,128]{3,0,2,1:T(8,128)S(1)} %get-tuple-element.12), channel_id=1, source_target_pairs={{4,0},{5,1},{6,2},{7,3},{12,8},{13,9},{14,10},{15,11},{20,16},{21,... | collective-permute-start | bytes 491528 | tf_op jit(solution)/shard_map/ppermute | solution.py:17
  204.8 2.2 copy-start.7
  206.8 0.7 copy-start.8
  211.7 9.5 %collective-permute-start.16 = (f32[32,10,10,1]{0,3,2,1:T(1,128)S(1)}, f32[32,10,10,1]{0,3,2,1:T(1,128)S(1)}, u32[]{:S(2)}, u32[]{:S(2)}) collective-permute-start(f32[32,10,10,1]{0,3,2,1:T(1,128)S(1)} %copy.21), channel_id=1, source_target_pairs={{1,0},{2,1},{3,2},{5,4},{6,5},{7,6},{9,8},{10,9},{11,10},{13,12},{... | collective-permute-start | bytes 38408 | tf_op jit(solution)/shard_map/ppermute | solution.py:17
  215.7 10.0 %copy-start.2 = (f32[32,8,8,128]{3,2,1,0:T(8,128)S(1)}, f32[32,8,8,128]{3,2,1,0:T(8,128)}, u32[]{:S(2)}) copy-start(f32[32,8,8,128]{3,2,1,0:T(8,128)} %param.8) | copy-start | bytes 3145732
  215.7 7.4 %collective-permute-start.17 = (f32[32,10,10,1]{0,3,2,1:T(1,128)}, f32[32,10,10,1]{0,3,2,1:T(1,128)}, u32[]{:S(2)}, u32[]{:S(2)}) collective-permute-start(f32[32,10,10,1]{0,3,2,1:T(1,128)} %copy.23), channel_id=1, source_target_pairs={{0,1},{1,2},{2,3},{4,5},{5,6},{6,7},{8,9},{9,10},{10,11},{12,13},{... | collective-permute-start | bytes 38408 | tf_op jit(solution)/shard_map/ppermute | solution.py:14
Sparse Core Ops, SparseCore 0:
  14.3 57.6 all-reduce.2
  74.9 41.2 all-reduce.4
